TPU v7x, 32 devices: a whole 2x2x4 slice. The times are simulated.
32 devices in a mesh: row: 8 (over z, core), col: 4 (over y, x).
Axes of the slice: x: 2, y: 2, z: 4, core: 2. Of those that a mesh axis runs over, the one named last changes fastest.
Arguments:
- loadings: bfloat16 [8, 32768, 1024], P(None, 'row', 'col'), may hold values from -6 to 6
- weights: bfloat16 [8, 32768, 512], P(None, 'row', 'col'), may hold values from -0.03125 to 0.03125
- specific: float32 [8, 32768], P(None, 'row'), may hold values from 0.2 to 5
- factor_cov: float32 [8, 1024, 1024], P(None, 'col'), may hold values from -0.001953125 to 0.0048828125, as said below
Outputs:
- portfolio_cov: float32 [8, 512, 512], P(None, 'row', 'col')
Inputs may be any that keep to these rules, and one draw needn't show every extreme that they name: `factor_cov`: each day's matrix is a symmetric positive definite factor covariance of order 1024.
All inputs are finite; a program needn't handle non-finite values.
Results may differ from a plain program's by a relative error of at most 0.0003.
Values may be sent and summed in bfloat16 or wider, within the bound.
No kernel may reach another device: no remote copies, remote signals or barrier semaphores. Data moves between devices by JAX's collectives and lax.ppermute only.
A program may use at most 128 MiB of HBM per device.

v0:
```python
import jax
import jax.numpy as jnp
from jax import lax
from jax.sharding import PartitionSpec as P


def shards(loadings, weights, specific, factor_cov):
    factor_cols = loadings.shape[2]
    port_cols = weights.shape[2]
    total_ports = port_cols * lax.axis_size("col")
    port_rows = total_ports // lax.axis_size("row")
    row_start = lax.axis_index("row") * port_rows
    weighted = (specific[:, :, None] * weights.astype(jnp.float32)).astype(jnp.bfloat16)
    fragment = lax.all_gather(weights, "col", axis=2, tiled=True)
    exposure_part = jnp.einsum(
        "dar,dap->drp", loadings, fragment, preferred_element_type=jnp.float32
    )
    specific_term = jnp.einsum(
        "dak,dap->dkp", weighted, fragment, preferred_element_type=jnp.float32
    )
    joined = jnp.concatenate([exposure_part, specific_term], axis=1)
    exposure = lax.psum(joined[:, :factor_cols, :], "row")
    specific_block = lax.psum_scatter(
        joined[:, factor_cols:, :], "row", scatter_dimension=2, tiled=True
    )
    exposure_rows = lax.dynamic_slice_in_dim(exposure, row_start, port_rows, 2)
    left_part = jnp.einsum(
        "dri,drs->dis", exposure_rows, factor_cov, precision=lax.Precision.HIGHEST
    )
    left = lax.psum(left_part, "col")
    exposure_cols = lax.all_to_all(exposure, "col", split_axis=2, concat_axis=1, tiled=True)
    factor_block = jnp.einsum("dir,drk->dik", left, exposure_cols, precision=lax.Precision.HIGHEST)
    return factor_block + jnp.swapaxes(specific_block, 1, 2)


def solution(mesh):
    in_specs = (P(None, "row", "col"), P(None, "row", "col"), P(None, "row"), P(None, "col", None))
    out_specs = P(None, "row", "col")
    return jax.shard_map(shards, mesh=mesh, in_specs=in_specs, out_specs=out_specs, check_vma=False)
```

profile of v0, /device:TPU:0, one launch (start us, length us, event | category | flops | bytes accessed | tf_op | source)
XLA Modules:
  0.0 558.4 jit_solution(18040227865551506382)
XLA Ops:
  6.5 0.0 all-gather.2.cloned.1.call-start
  6.5 0.7 all-gather.2.cloned.1.call-update
  7.3 0.0 copy-start
  7.3 0.0 all-reduce.3.cloned.1.call-start
  7.3 301.6 %all-gather.2.cloned.1.call-done = bf16[8,4096,512]{2,1,0:T(8,128)(2,1)} async-done(((bf16[8,4096,128]{2,1,0:T(8,128)(2,1)}), bf16[8,4096,512]{2,1,0:T(8,128)(2,1)}) %all-gather.2.cloned.1.call-update) | async-done | bytes 33554448 | tf_op jit(solution)/shard_map/all_gather | solution.py:14
  308.9 21.1 %fusion.5 = f32[8,256,512]{2,1,0:T(8,128)} fusion(bf16[8,4096,256]{2,1,0:T(8,128)(2,1)} %param.4, bf16[8,4096,512]{2,1,0:T(8,128)(2,1)} %all-gather.2.cloned.1.call-done), kind=kOutput, calls=%fused_computation.7 | convolution fusion | flops 8589934592 | bytes 54525952 | tf_op jit(solution)/shard_map/dar,dap->drp/dot_general | solution.py:15
  329.9 0.0 all-reduce.3.cloned.1.call-update
  330.0 0.0 reduce-scatter.2.cloned.1.call-start
  330.0 0.0 copy-done
  330.0 21.5 %fusion = f32[8,128,512]{1,2,0:T(8,128)} fusion(bf16[8,4096,512]{2,1,0:T(8,128)(2,1)} %all-gather.2.cloned.1.call-done, bf16[8,4096,128]{2,1,0:T(8,128)(2,1)} %param.5, f32[8,4096]{1,0:T(8,128)S(1)} %copy-done), kind=kOutput, calls=%fused_computation.1 | convolution fusion | flops 4307550208 | bytes 44171264 | tf_op jit(solution)/shard_map/dak,dap->dkp/dot_general | solution.py:18
  351.5 0.0 reduce-scatter.2.cloned.1.call-update
  351.5 75.1 %all-reduce.3.cloned.1.call-done = f32[8,256,512]{2,1,0:T(8,128)} async-done(((f32[8,256,512]{2,1,0:T(8,128)}), f32[8,256,512]{2,1,0:T(8,128)}) %all-reduce.3.cloned.1.call-update) | async-done | bytes 4194320 | tf_op jit(solution)/shard_map/psum | solution.py:22
  426.6 5.5 copy.9
  432.1 5.0 all-to-all-start
  437.1 0.2 all-reduce.5.cloned.1.call-start
  437.3 10.4 %fusion.2 = f32[8,64,1024]{2,1,0:T(8,128)} fusion(f32[8,256,1024]{2,1,0:T(8,128)} %param.7, f32[8,256,512]{2,1,0:T(8,128)} %all-reduce.3.cloned.1.call-done, s32[]{:T(128)S(6)} %select_n.3), kind=kOutput, calls=%fused_computation.4 | convolution fusion | flops 1610612736 | bytes 11534340 | tf_op jit(solution)/shard_map/dri,drs->dis/dot_general | solution.py:27
  447.7 0.0 all-reduce.5.cloned.1.call-update
  447.7 47.9 %all-to-all-done = f32[8,256,512]{1,0,2:T(8,128)} async-done(((f32[8,256,512]{1,0,2:T(8,128)}), f32[8,256,512]{1,0,2:T(8,128)}, u32[]{:S(2)}, u32[]{:S(2)}) %all-to-all-start) | async-done | bytes 4194336 | tf_op jit(solution)/shard_map/all_to_all | solution.py:31
  495.6 5.3 copy.10
  500.9 0.0 reduce-scatter.2.cloned.1.call-done
  500.9 44.7 %all-reduce.5.cloned.1.call-done = f32[8,64,1024]{2,1,0:T(8,128)} async-done(((f32[8,64,1024]{2,1,0:T(8,128)}), f32[8,64,1024]{2,1,0:T(8,128)}) %all-reduce.5.cloned.1.call-update) | async-done | bytes 2097168 | tf_op jit(solution)/shard_map/psum | solution.py:30
  545.7 6.2 %convolution_add_fusion = f32[8,64,128]{2,1,0:T(8,128)} fusion(f32[8,64,1024]{2,1,0:T(8,128)} %all-reduce.5.cloned.1.call-done, f32[8,1024,128]{2,1,0:T(8,128)} %bitcast.12, f32[8,128,64]{1,2,0:T(8,128)} %reduce-scatter.2.cloned.1.call-done), kind=kOutput, calls=%fused_computation.3 | convolution fusion | flops 805371904 | bytes 6815744 | tf_op jit(solution)/shard_map/dir,drk->dik/dot_general | solution.py:32
Async XLA Ops:
  6.5 302.3 %all-gather.2.cloned.1.call-start = ((), (), s32[]{:S(2)}) async-start(), calls=%async_computation.2 | async-start | bytes 41943040 | tf_op jit(solution)/shard_map/all_gather | solution.py:14
  7.3 322.8 %copy-start = (f32[8,4096]{1,0:T(8,128)S(1)}, f32[8,4096]{1,0:T(8,128)}, u32[]{:S(2)}) copy-start(f32[8,4096]{1,0:T(8,128)} %param.6) | copy-start | bytes 393220
  7.3 419.3 %all-reduce.3.cloned.1.call-start = ((), (), s32[]{:S(2)}) async-start(), calls=%async_computation.3 | async-start | bytes 8388608 | tf_op jit(solution)/shard_map/psum | solution.py:22
  330.0 171.0 %reduce-scatter.2.cloned.1.call-start = ((), (), s32[]{:S(2)}) async-start(), calls=%async_computation.5 | async-start | bytes 2359296 | tf_op jit(solution)/shard_map/reduce_scatter | solution.py:23
  432.1 63.5 %all-to-all-start = ((f32[8,256,512]{1,0,2:T(8,128)}), f32[8,256,512]{1,0,2:T(8,128)}, u32[]{:S(2)}, u32[]{:S(2)}) async-start(f32[8,256,512]{1,0,2:T(8,128)} %copy.9), calls=%async_computation | async-start | bytes 8388608 | tf_op jit(solution)/shard_map/all_to_all | solution.py:31
  437.1 108.6 %all-reduce.5.cloned.1.call-start = ((), (), s32[]{:S(2)}) async-start(), calls=%async_computation.4 | async-start | bytes 4194304 | tf_op jit(solution)/shard_map/psum | solution.py:30
Sparse Core Ops, SparseCore 0:
  9.2 299.6 all-gather.1
  330.1 96.4 all-reduce.2
  428.9 36.0 reduce-scatter.1
  468.0 77.6 all-reduce.4
where the time goes:
time: 559 us; the launch traced here: 558 us
  waiting for transfers between devices  470 us (84%)
  matrix products  59.1 us (11%)
  between operations  13.2 us (2%)
  local copies, waits for them, and re-layouts  10.8 us (2%)
    all_gather x1, waiting for transfers between devices, shards(): fragment = lax.all_gather(weights, 'col', axis=2, tiled=True)  302 us
    psum x1, waiting for transfers between devices, shards(): exposure = lax.psum(joined[:, :factor_cols, :], 'row')  75.1 us
    all_to_all x1, waiting for transfers between devices, shards(): lax.all_to_all(exposure, 'col', split_axis=2, concat_axis=1, tiled=True)  47.9 us
    psum x1, waiting for transfers between devices, shards(): left = lax.psum(left_part, 'col')  44.7 us
    dot_general x1, matrix products, shards(): jnp.einsum('dak,dap->dkp', weighted, fragment, preferred_element_type=jnp...  21.5 us
    dot_general x1, matrix products, shards(): jnp.einsum('dar,dap->drp', loadings, fragment, preferred_element_type=jnp...  21.1 us
  transfers between devices with their start and end apart: 5, of which 4 were waited for; matrix products, arithmetic and copies ran while one was open for 8% of the time, Pallas kernels for 0%

commit v1 on v0

v1 whole, which is shorter than its diff:
```python
import jax
import jax.numpy as jnp
from jax import lax
from jax.sharding import PartitionSpec as P

HIGH = lax.Precision.HIGHEST


def powers(count):
    return [1 << t for t in range(count.bit_length() - 1)]


def swap(x, axis, bit):
    size = lax.axis_size(axis)
    return lax.ppermute(x, axis, [(i, i ^ bit) for i in range(size)])


def bit_of(index, bit):
    return (index // bit) % 2


def pick(x, where, axis):
    return lax.dynamic_index_in_dim(x, where, axis, keepdims=False)


def contract(left, right):
    return lax.dot_general(left, right, (((0,), (0,)), ((), ())), preferred_element_type=jnp.float32)


def spread(pieces, bits):
    for bit in bits:
        for j in list(pieces):
            pieces[j ^ bit] = swap(pieces[j], "col", bit)
    return jnp.concatenate([pieces[j] for j in sorted(pieces)], axis=1)


def scaled(specific, weights):
    return (specific[:, None] * weights.astype(jnp.float32)).astype(jnp.bfloat16)


def partial_merged(loadings, weights, specific, order):
    bit = order[0]
    mine = bit_of(lax.axis_index("col"), bit)
    halves = [a.reshape((2, a.shape[0] // 2) + a.shape[1:]) for a in (loadings, weights, specific)]
    kept = [pick(a, mine, 0) for a in halves]
    load_in, weight_in = [swap(pick(a, 1 - mine, 0), "col", bit) for a in halves[:2]]
    everyone = spread({0: kept[1], bit: weight_in}, order[1:])
    own = jnp.concatenate([kept[1], weight_in], axis=1)
    right = jnp.concatenate([kept[0], load_in, scaled(kept[2], own)], axis=1)
    return contract(everyone, right)


def partial_static(loadings, weights, specific, order):
    half = loadings.shape[0] // 2
    total = None
    for part, bits in ((slice(0, half), order), (slice(half, None), order[::-1])):
        everyone = spread({0: weights[part]}, bits)
        right = jnp.concatenate([loadings[part], scaled(specific[part], weights[part])], axis=1)
        term = contract(everyone, right)
        total = term if total is None else total + term
    return total


def row_reduce(x):
    rows, cols = lax.axis_size("row"), lax.axis_size("col")
    row, col = lax.axis_index("row"), lax.axis_index("col")
    subs = rows // cols
    days, ports, width = x.shape
    x = x.reshape((days,) + (2,) * (rows.bit_length() - 1) + (ports // rows, width))
    for bit in powers(rows):
        keep = bit_of(row, bit)
        if bit >= subs:
            keep = keep ^ bit_of(col, bit // subs)
        axis = x.ndim - 3
        x = pick(x, keep, axis) + swap(pick(x, 1 - keep, axis), "row", bit)
    return x


def finish(sums, orders, merged, factor_cov):
    rows, cols = lax.axis_size("row"), lax.axis_size("col")
    row, col = lax.axis_index("row"), lax.axis_index("col")
    subs = rows // cols
    factors = factor_cov[0].shape[0]
    own, specific, whole = [], [], []
    for x, order, both in zip(sums, orders, merged):
        if both:
            bit, rest = order[0], order[1:]
            one, two, ports = x[:, :factors], x[:, factors : 2 * factors], (x.shape[1] - 2 * factors) // 2
            there = jnp.concatenate([two, one, x[:, 2 * factors + ports :]], axis=1)
            x = x[:, : 2 * factors + ports] + swap(there, "col", bit)
            blocks = jnp.stack([x[:, :factors], x[:, factors : 2 * factors]])
            names = [0, bit]
            specific.append(x[:, 2 * factors :])
        else:
            rest = order
            blocks, names = x[None, :, :factors], [0]
            specific.append(x[:, factors:])
        own.append(blocks[0])
        for bit in rest:
            blocks = jnp.concatenate([blocks, swap(blocks, "col", bit)])
            names = names + [name ^ bit for name in names]
        blocks = jnp.stack([blocks[names.index(j)] for j in range(cols)])
        whole.append(jnp.concatenate([pick(blocks, col ^ j, 0) for j in range(cols)], axis=1))
    every = jnp.stack(own)
    for bit in powers(rows)[::-1]:
        every = jnp.stack([every, swap(every, "row", bit)], axis=every.ndim - 2)
    every = every.reshape(len(own), -1, factors)
    outs = []
    for t, order in enumerate(orders):
        left = lax.dot_general(whole[t], factor_cov[t], (((1,), (1,)), ((), ())), precision=HIGH)
        part = lax.dot_general(left, every[t], (((1,), (1,)), ((), ())), precision=HIGH)
        lines, ports = part.shape[0], part.shape[1] // cols
        part = jnp.stack([part[:, q * ports : (q + 1) * ports] for q in range(cols)])
        part = part.reshape((2,) * (cols.bit_length() - 1) + (lines, ports))
        left_bits = powers(cols)
        for bit in order:
            keep = bit_of(row // subs, bit) ^ bit_of(col, bit)
            axis = len(left_bits) - 1 - left_bits.index(bit)
            left_bits.remove(bit)
            part = pick(part, keep, axis) + swap(pick(part, 1 - keep, axis), "col", bit)
        part = part.reshape((lines, subs, ports // subs))
        part = jnp.concatenate([pick(part, (row % subs) ^ s, 1) for s in range(subs)], axis=1)
        outs.append(part + specific[t])
    return outs


def groups_of(days, bits):
    order = list(bits)
    late = days - 2
    groups = [[(d, order if d % 2 == 0 else order[::-1], True) for d in range(s, min(s + 2, late))] for s in range(0, late, 2)]
    return groups + [[(d, order, False)] for d in range(max(late, 0), days)]


def shards(loadings, weights, specific, factor_cov):
    results = {}
    for group in groups_of(loadings.shape[0], powers(lax.axis_size("col"))):
        parts = []
        for d, order, both in group:
            build = partial_merged if both else partial_static
            parts.append(build(loadings[d], weights[d], specific[d], order))
        sums = row_reduce(jnp.stack(parts))
        days = [d for d, _, _ in group]
        outs = finish([sums[t] for t in range(len(days))], [g[1] for g in group], [g[2] for g in group], [factor_cov[d] for d in days])
        results.update(zip(days, outs))
    return jnp.stack([results[d] for d in sorted(results)])


def solution(mesh):
    in_specs = (P(None, "row", "col"), P(None, "row", "col"), P(None, "row"), P(None, "col", None))
    out_specs = P(None, "row", "col")
    return jax.shard_map(shards, mesh=mesh, in_specs=in_specs, out_specs=out_specs, check_vma=False)
```

time: 559 us -> 499 us (0.89)
  waiting for transfers between devices: 470 us -> 295 us
  starting transfers between devices: 5.27 us -> 88.6 us
  local copies, waits for them, and re-layouts: 10.8 us -> 48.6 us
  other arithmetic: 0 us -> 22.4 us
  matrix products: 59.1 us -> 37.4 us
  between operations: 13.2 us -> 2.67 us
    all_gather x1 -> x0, waiting for transfers between devices: 302 us -> none  [shards(): fragment = lax.all_gather(weights, 'col', axis=2, tiled=True)]
    ppermute x0 -> x98, waiting for transfers between devices: none -> 295 us  [swap(): return lax.ppermute(x, axis, [(i, i ^ bit) for i in range(size)])]
    psum x2 -> x0, waiting for transfers between devices: 120 us -> none  [the longest x1 75.1 us: shards(): exposure = lax.psum(joined[:, :factor_cols, :], 'row')]
    ppermute x0 -> x98, starting transfers between devices: none -> 88.6 us  [swap(): return lax.ppermute(x, axis, [(i, i ^ bit) for i in range(size)])]
    all_to_all x1 -> x0, waiting for transfers between devices: 47.9 us -> none  [shards(): lax.all_to_all(exposure, 'col', split_axis=2, concat_axis=1, tiled=True)]
    squeeze x0 -> x48, local copies, waits for them, and re-layouts: none -> 22.8 us  [the longest x45 22.7 us: pick(): return lax.dynamic_index_in_dim(x, where, axis, keepdims=False)]
    dot_general x4 -> x26, matrix products: 59.1 us -> 37.4 us  [the longest x10 21.4 us: contract(): lax.dot_general(left, right, (((0,), (0,)), ((), ())), preferred_element_...]
    slice x0 -> x25, local copies, waits for them, and re-layouts: none -> 21.1 us  [the longest x3 13.7 us: shards(): parts.append(build(loadings[d], weights[d], specific[d], order))]
  transfers between devices with their start and end apart: 5 -> 98, of which waited for: 4 -> 43; matrix products, arithmetic and copies ran while one was open for 8% -> 21% of each run, Pallas kernels for 0% -> 0%
where the time goes in v1:
time: 499 us; the launch traced here: 495 us
  waiting for transfers between devices  295 us (59%)
  starting transfers between devices  88.6 us (18%)
  local copies, waits for them, and re-layouts  48.6 us (10%)
  matrix products  37.4 us (7%)
  other arithmetic  22.4 us (4%)
    ppermute x98, waiting for transfers between devices, swap(): return lax.ppermute(x, axis, [(i, i ^ bit) for i in range(size)])  295 us
    ppermute x98, starting transfers between devices, swap(): return lax.ppermute(x, axis, [(i, i ^ bit) for i in range(size)])  88.6 us
    squeeze x45, local copies, waits for them, and re-layouts, pick(): return lax.dynamic_index_in_dim(x, where, axis, keepdims=False)  22.7 us
    dot_general x10, matrix products, contract(): lax.dot_general(left, right, (((0,), (0,)), ((), ())), preferred_element_...  21.4 us
    slice x3, local copies, waits for them, and re-layouts, shards(): parts.append(build(loadings[d], weights[d], specific[d], order))  13.7 us
    dot_general x8, matrix products, finish(): lax.dot_general(whole[t], factor_cov[t], (((1,), (1,)), ((), ())), precis...  11.2 us
    convert_element_type x7, other arithmetic, scaled(): (specific[:, None] * weights.astype(jnp.float32)).astype(jnp.bfloat16)  10.2 us
  transfers between devices with their start and end apart: 98, of which 43 were waited for; matrix products, arithmetic and copies ran while one was open for 21% of the time, Pallas kernels for 0%

profile of v1, /device:TPU:0, one launch (start us, length us, event | category | flops | bytes accessed | tf_op | source)
XLA Modules:
  0.0 494.8 jit_solution(10984717197852333244)
XLA Ops:
  7.4 4.6 fusion.304
  19.2 8.8 %fusion.303 = (bf16[1,4096,256]{2,1,0:T(8,128)(2,1)S(1)}, bf16[1,4096,256]{2,1,0:T(8,128)(2,1)}, bf16[1,4096,256]{2,1,0:T(8,128)(2,1)}, bf16[1,4096,256]{2,1,0:T...) fusion(bf16[8,4096,256]{2,1,0:T(8,128)(2,1)} %param.4), kind=kLoop, calls=%fused_computation.593 | loop fusion | bytes 25165824 | tf_op jit(solution)/shard_map/slice | solution.py:140
  28.1 4.2 slice_bitcast_fusion.1
  48.9 4.8 multiply_convert_fusion.7
  62.1 8.1 %collective-permute-done.27 = bf16[2048,128]{1,0:T(8,128)(2,1)S(1)} collective-permute-done((bf16[2048,128]{1,0:T(8,128)(2,1)S(1)}, bf16[2048,128]{1,0:T(8,128)(2,1)S(1)}, u32[]{:S(2)}, u32[]{:S(2)}) %collective-permute-start.27) | collective-permute-done | bytes 524320 | tf_op jit(solution)/shard_map/ppermute | solution.py:15
  74.6 6.9 %collective-permute-done.49 = bf16[2048,128]{1,0:T(8,128)(2,1)S(1)} collective-permute-done((bf16[2048,128]{1,0:T(8,128)(2,1)S(1)}, bf16[2048,128]{1,0:T(8,128)(2,1)S(1)}, u32[]{:S(2)}, u32[]{:S(2)}) %collective-permute-start.49) | collective-permute-done | bytes 524320 | tf_op jit(solution)/shard_map/ppermute | solution.py:15
  86.9 9.4 %collective-permute-done.71 = bf16[2048,128]{1,0:T(8,128)(2,1)S(1)} collective-permute-done((bf16[2048,128]{1,0:T(8,128)(2,1)}, bf16[2048,128]{1,0:T(8,128)(2,1)S(1)}, u32[]{:S(2)}, u32[]{:S(2)}) %collective-permute-start.71) | collective-permute-done | bytes 524320 | tf_op jit(solution)/shard_map/ppermute | solution.py:15
  104.0 3.5 collective-permute-done.82
  107.6 7.6 %collective-permute-done.68 = bf16[2048,128]{1,0:T(8,128)(2,1)S(1)} collective-permute-done((bf16[2048,128]{1,0:T(8,128)(2,1)S(1)}, bf16[2048,128]{1,0:T(8,128)(2,1)S(1)}, u32[]{:S(2)}, u32[]{:S(2)}) %collective-permute-start.68) | collective-permute-done | bytes 524320 | tf_op jit(solution)/shard_map/ppermute | solution.py:15
  120.3 29.5 %collective-permute-done.87 = bf16[2048,128]{1,0:T(8,128)(2,1)S(1)} collective-permute-done((bf16[2048,128]{1,0:T(8,128)(2,1)S(1)}, bf16[2048,128]{1,0:T(8,128)(2,1)S(1)}, u32[]{:S(2)}, u32[]{:S(2)}) %collective-permute-start.87) | collective-permute-done | bytes 524320 | tf_op jit(solution)/shard_map/ppermute | solution.py:15
  158.2 30.3 %collective-permute-done.2 = bf16[2048,128]{1,0:T(8,128)(2,1)S(1)} collective-permute-done((bf16[2048,128]{1,0:T(8,128)(2,1)}, bf16[2048,128]{1,0:T(8,128)(2,1)S(1)}, u32[]{:S(2)}, u32[]{:S(2)}) %collective-permute-start.2) | collective-permute-done | bytes 524320 | tf_op jit(solution)/shard_map/ppermute | solution.py:15
  195.5 7.4 %collective-permute-done.6 = bf16[2048,128]{1,0:T(8,128)(2,1)S(1)} collective-permute-done((bf16[2048,128]{1,0:T(8,128)(2,1)}, bf16[2048,128]{1,0:T(8,128)(2,1)S(1)}, u32[]{:S(2)}, u32[]{:S(2)}) %collective-permute-start.6) | collective-permute-done | bytes 524320 | tf_op jit(solution)/shard_map/ppermute | solution.py:15
  209.6 23.8 %collective-permute-done.24 = bf16[2048,128]{1,0:T(8,128)(2,1)S(1)} collective-permute-done((bf16[2048,128]{1,0:T(8,128)(2,1)}, bf16[2048,128]{1,0:T(8,128)(2,1)S(1)}, u32[]{:S(2)}, u32[]{:S(2)}) %collective-permute-start.24) | collective-permute-done | bytes 524320 | tf_op jit(solution)/shard_map/ppermute | solution.py:15
  240.7 7.5 %collective-permute-done.28 = bf16[2048,128]{1,0:T(8,128)(2,1)S(1)} collective-permute-done((bf16[2048,128]{1,0:T(8,128)(2,1)S(1)}, bf16[2048,128]{1,0:T(8,128)(2,1)S(1)}, u32[]{:S(2)}, u32[]{:S(2)}) %collective-permute-start.28) | collective-permute-done | bytes 524320 | tf_op jit(solution)/shard_map/ppermute | solution.py:15
  254.0 20.4 %collective-permute-done.46 = bf16[2048,128]{1,0:T(8,128)(2,1)S(1)} collective-permute-done((bf16[2048,128]{1,0:T(8,128)(2,1)S(1)}, bf16[2048,128]{1,0:T(8,128)(2,1)S(1)}, u32[]{:S(2)}, u32[]{:S(2)}) %collective-permute-start.46) | collective-permute-done | bytes 524320 | tf_op jit(solution)/shard_map/ppermute | solution.py:15
  283.2 5.6 %collective-permute-done.73 = f32[1,2,64,384]{3,2,1,0:T(8,128)S(1)} collective-permute-done((f32[1,2,64,384]{3,2,1,0:T(8,128)S(1)}, f32[1,2,64,384]{3,2,1,0:T(8,128)S(1)}, u32[]{:S(2)}, u32[]{:S(2)}) %collective-permute-start.73) | collective-permute-done | bytes 196640 | tf_op jit(solution)/shard_map/ppermute | solution.py:15
  300.8 4.8 collective-permute-done.77
  307.6 4.9 collective-permute-done.93
  312.9 4.6 collective-permute-done.76
  350.3 15.6 %collective-permute-done.9 = f32[2,2,64,768]{3,2,0,1:T(8,128)S(1)} collective-permute-done((f32[2,2,64,768]{3,2,0,1:T(8,128)S(1)}, f32[2,2,64,768]{3,2,0,1:T(8,128)S(1)}, u32[]{:S(2)}, u32[]{:S(2)}) %collective-permute-start.9) | collective-permute-done | bytes 786464 | tf_op jit(solution)/shard_map/ppermute | solution.py:15
  366.2 25.0 %collective-permute-done.31 = f32[2,2,64,768]{3,2,0,1:T(8,128)S(1)} collective-permute-done((f32[2,2,64,768]{3,2,0,1:T(8,128)S(1)}, f32[2,2,64,768]{3,2,0,1:T(8,128)S(1)}, u32[]{:S(2)}, u32[]{:S(2)}) %collective-permute-start.31) | collective-permute-done | bytes 786464 | tf_op jit(solution)/shard_map/ppermute | solution.py:15
  391.4 15.4 %collective-permute-done.53 = f32[2,2,64,768]{3,2,0,1:T(8,128)S(1)} collective-permute-done((f32[2,2,64,768]{3,2,0,1:T(8,128)S(1)}, f32[2,2,64,768]{3,2,0,1:T(8,128)S(1)}, u32[]{:S(2)}, u32[]{:S(2)}) %collective-permute-start.53) | collective-permute-done | bytes 786464 | tf_op jit(solution)/shard_map/ppermute | solution.py:15
  407.2 19.8 %collective-permute-done.32 = f32[2,64,768]{2,1,0:T(8,128)S(1)} collective-permute-done((f32[2,64,768]{2,1,0:T(8,128)S(1)}, f32[2,64,768]{2,1,0:T(8,128)S(1)}, u32[]{:S(2)}, u32[]{:S(2)}) %collective-permute-start.32) | collective-permute-done | bytes 393248 | tf_op jit(solution)/shard_map/ppermute | solution.py:15
  427.2 5.0 %collective-permute-done.54 = f32[2,64,768]{2,1,0:T(8,128)S(1)} collective-permute-done((f32[2,64,768]{2,1,0:T(8,128)S(1)}, f32[2,64,768]{2,1,0:T(8,128)S(1)}, u32[]{:S(2)}, u32[]{:S(2)}) %collective-permute-start.54) | collective-permute-done | bytes 393248 | tf_op jit(solution)/shard_map/ppermute | solution.py:15
  (516 shorter events, 214.4 us)
Async XLA Ops:
  2.9 70.3 %collective-permute-start.70 = (bf16[2048,128]{1,0:T(8,128)(2,1)}, bf16[2048,128]{1,0:T(8,128)(2,1)}, u32[]{:S(2)}, u32[]{:S(2)}) collective-permute-start(bf16[2048,128]{1,0:T(8,128)(2,1)} %get-tuple-element.22), channel_id=1, source_target_pairs={{0,2},{1,3},{2,0},{3,1},{4,6},{5,7},{6,4},{7,5},{8,10},{9,11},{10,... | collective-permute-start | bytes 1572872 | tf_op jit(solution)/shard_map/ppermute | solution.py:15
  5.9 77.1 %collective-permute-start.69 = (bf16[2048,128]{1,0:T(8,128)(2,1)}, bf16[2048,128]{1,0:T(8,128)(2,1)}, u32[]{:S(2)}, u32[]{:S(2)}) collective-permute-start(bf16[2048,128]{1,0:T(8,128)(2,1)} %get-tuple-element.22), channel_id=1, source_target_pairs={{0,1},{1,0},{2,3},{3,2},{4,5},{5,4},{6,7},{7,6},{8,9},{9,8},{10,11... | collective-permute-start | bytes 1572872 | tf_op jit(solution)/shard_map/ppermute | solution.py:15
  14.3 41.1 %collective-permute-start = (bf16[2048,128]{1,0:T(8,128)(2,1)}, bf16[2048,128]{1,0:T(8,128)(2,1)}, u32[]{:S(2)}, u32[]{:S(2)}) collective-permute-start(bf16[2048,128]{1,0:T(8,128)(2,1)} %get-tuple-element.70), channel_id=1, source_target_pairs={{0,1},{1,0},{2,3},{3,2},{4,5},{5,4},{6,7},{7,6},{8,9},{9,8},{10,11... | collective-permute-start | bytes 1572872 | tf_op jit(solution)/shard_map/ppermute | solution.py:15
  15.9 42.6 %collective-permute-start.5 = (bf16[2048,128]{1,0:T(8,128)(2,1)}, bf16[2048,128]{1,0:T(8,128)(2,1)}, u32[]{:S(2)}, u32[]{:S(2)}) collective-permute-start(bf16[2048,128]{1,0:T(8,128)(2,1)} %get-tuple-element.68), channel_id=1, source_target_pairs={{0,2},{1,3},{2,0},{3,1},{4,6},{5,7},{6,4},{7,5},{8,10},{9,11},{10,... | collective-permute-start | bytes 1572872 | tf_op jit(solution)/shard_map/ppermute | solution.py:15
  16.9 43.6 %collective-permute-start.22 = (bf16[2048,128]{1,0:T(8,128)(2,1)}, bf16[2048,128]{1,0:T(8,128)(2,1)}, u32[]{:S(2)}, u32[]{:S(2)}) collective-permute-start(bf16[2048,128]{1,0:T(8,128)(2,1)} %get-tuple-element.64), channel_id=1, source_target_pairs={{0,1},{1,0},{2,3},{3,2},{4,5},{5,4},{6,7},{7,6},{8,9},{9,8},{10,11... | collective-permute-start | bytes 1572872 | tf_op jit(solution)/shard_map/ppermute | solution.py:15
  99.1 52.0 %collective-permute-start.83 = (bf16[2048,128]{1,0:T(8,128)(2,1)S(1)}, bf16[2048,128]{1,0:T(8,128)(2,1)S(1)}, u32[]{:S(2)}, u32[]{:S(2)}) collective-permute-start(bf16[2048,128]{1,0:T(8,128)(2,1)S(1)} %copy-done.38), channel_id=1, source_target_pairs={{0,2},{1,3},{2,0},{3,1},{4,6},{5,7},{6,4},{7,5},{8,10},{9,11},{10,... | collective-permute-start | bytes 1572872 | tf_op jit(solution)/shard_map/ppermute | solution.py:15
  104.0 52.6 %collective-permute-start.3 = (bf16[2048,256]{1,0:T(8,128)(2,1)S(1)}, bf16[2048,256]{1,0:T(8,128)(2,1)S(1)}, u32[]{:S(2)}, u32[]{:S(2)}) collective-permute-start(bf16[2048,256]{1,0:T(8,128)(2,1)S(1)} %copy-done.30), channel_id=1, source_target_pairs={{0,1},{1,0},{2,3},{3,2},{4,5},{5,4},{6,7},{7,6},{8,9},{9,8},{10,11... | collective-permute-start | bytes 3145736 | tf_op jit(solution)/shard_map/ppermute | solution.py:15
  107.5 42.2 %collective-permute-start.87 = (bf16[2048,128]{1,0:T(8,128)(2,1)S(1)}, bf16[2048,128]{1,0:T(8,128)(2,1)S(1)}, u32[]{:S(2)}, u32[]{:S(2)}) collective-permute-start(bf16[2048,128]{1,0:T(8,128)(2,1)S(1)} %collective-permute-done.86), channel_id=1, source_target_pairs={{0,1},{1,0},{2,3},{3,2},{4,5},{5,4},{6,7},{7,6},{8,9},{9,8},{10,11... | collective-permute-start | bytes 1572872 | tf_op jit(solution)/shard_map/ppermute | solution.py:15
  115.2 37.9 %collective-permute-start.84 = (bf16[2048,128]{1,0:T(8,128)(2,1)S(1)}, bf16[2048,128]{1,0:T(8,128)(2,1)S(1)}, u32[]{:S(2)}, u32[]{:S(2)}) collective-permute-start(bf16[2048,128]{1,0:T(8,128)(2,1)S(1)} %collective-permute-done.82), channel_id=1, source_target_pairs={{0,2},{1,3},{2,0},{3,1},{4,6},{5,7},{6,4},{7,5},{8,10},{9,11},{10,... | collective-permute-start | bytes 1572872 | tf_op jit(solution)/shard_map/ppermute | solution.py:15
  149.8 43.8 %collective-permute-start.4 = (bf16[2048,128]{1,0:T(8,128)(2,1)S(1)}, bf16[2048,128]{1,0:T(8,128)(2,1)S(1)}, u32[]{:S(2)}, u32[]{:S(2)}) collective-permute-start(bf16[2048,128]{1,0:T(8,128)(2,1)S(1)} %copy-done.17), channel_id=1, source_target_pairs={{0,1},{1,0},{2,3},{3,2},{4,5},{5,4},{6,7},{7,6},{8,9},{9,8},{10,11... | collective-permute-start | bytes 1572872 | tf_op jit(solution)/shard_map/ppermute | solution.py:15
  151.1 42.5 %collective-permute-start.7 = (bf16[2048,256]{1,0:T(8,128)(2,1)S(1)}, bf16[2048,256]{1,0:T(8,128)(2,1)S(1)}, u32[]{:S(2)}, u32[]{:S(2)}) collective-permute-start(bf16[2048,256]{1,0:T(8,128)(2,1)S(1)} %copy-done.28), channel_id=1, source_target_pairs={{0,2},{1,3},{2,0},{3,1},{4,6},{5,7},{6,4},{7,5},{8,10},{9,11},{10,... | collective-permute-start | bytes 3145736 | tf_op jit(solution)/shard_map/ppermute | solution.py:15
  154.6 52.7 %collective-permute-start.23 = (bf16[2048,128]{1,0:T(8,128)(2,1)S(1)}, bf16[2048,128]{1,0:T(8,128)(2,1)S(1)}, u32[]{:S(2)}, u32[]{:S(2)}) collective-permute-start(bf16[2048,128]{1,0:T(8,128)(2,1)S(1)} %copy-done.15), channel_id=1, source_target_pairs={{0,2},{1,3},{2,0},{3,1},{4,6},{5,7},{6,4},{7,5},{8,10},{9,11},{10,... | collective-permute-start | bytes 1572872 | tf_op jit(solution)/shard_map/ppermute | solution.py:15
  156.6 52.7 %collective-permute-start.25 = (bf16[2048,256]{1,0:T(8,128)(2,1)S(1)}, bf16[2048,256]{1,0:T(8,128)(2,1)S(1)}, u32[]{:S(2)}, u32[]{:S(2)}) collective-permute-start(bf16[2048,256]{1,0:T(8,128)(2,1)S(1)} %copy-done.26), channel_id=1, source_target_pairs={{0,1},{1,0},{2,3},{3,2},{4,5},{5,4},{6,7},{7,6},{8,9},{9,8},{10,11... | collective-permute-start | bytes 3145736 | tf_op jit(solution)/shard_map/ppermute | solution.py:15
  193.5 45.1 %collective-permute-start.26 = (bf16[2048,128]{1,0:T(8,128)(2,1)S(1)}, bf16[2048,128]{1,0:T(8,128)(2,1)S(1)}, u32[]{:S(2)}, u32[]{:S(2)}) collective-permute-start(bf16[2048,128]{1,0:T(8,128)(2,1)S(1)} %copy-done.16), channel_id=1, source_target_pairs={{0,1},{1,0},{2,3},{3,2},{4,5},{5,4},{6,7},{7,6},{8,9},{9,8},{10,11... | collective-permute-start | bytes 1572872 | tf_op jit(solution)/shard_map/ppermute | solution.py:15
  193.6 45.1 %collective-permute-start.29 = (bf16[2048,256]{1,0:T(8,128)(2,1)S(1)}, bf16[2048,256]{1,0:T(8,128)(2,1)S(1)}, u32[]{:S(2)}, u32[]{:S(2)}) collective-permute-start(bf16[2048,256]{1,0:T(8,128)(2,1)S(1)} %copy-done.24), channel_id=1, source_target_pairs={{0,2},{1,3},{2,0},{3,1},{4,6},{5,7},{6,4},{7,5},{8,10},{9,11},{10,... | collective-permute-start | bytes 3145736 | tf_op jit(solution)/shard_map/ppermute | solution.py:15
  207.2 44.7 %collective-permute-start.45 = (bf16[2048,128]{1,0:T(8,128)(2,1)S(1)}, bf16[2048,128]{1,0:T(8,128)(2,1)S(1)}, u32[]{:S(2)}, u32[]{:S(2)}) collective-permute-start(bf16[2048,128]{1,0:T(8,128)(2,1)S(1)} %copy-done.14), channel_id=1, source_target_pairs={{0,2},{1,3},{2,0},{3,1},{4,6},{5,7},{6,4},{7,5},{8,10},{9,11},{10,... | collective-permute-start | bytes 1572872 | tf_op jit(solution)/shard_map/ppermute | solution.py:15
  209.3 44.7 %collective-permute-start.47 = (bf16[2048,256]{1,0:T(8,128)(2,1)S(1)}, bf16[2048,256]{1,0:T(8,128)(2,1)S(1)}, u32[]{:S(2)}, u32[]{:S(2)}) collective-permute-start(bf16[2048,256]{1,0:T(8,128)(2,1)S(1)} %copy-done.21), channel_id=1, source_target_pairs={{0,1},{1,0},{2,3},{3,2},{4,5},{5,4},{6,7},{7,6},{8,9},{9,8},{10,11... | collective-permute-start | bytes 3145736 | tf_op jit(solution)/shard_map/ppermute | solution.py:15
  238.8 38.0 %collective-permute-start.51 = (bf16[2048,256]{1,0:T(8,128)(2,1)S(1)}, bf16[2048,256]{1,0:T(8,128)(2,1)S(1)}, u32[]{:S(2)}, u32[]{:S(2)}) collective-permute-start(bf16[2048,256]{1,0:T(8,128)(2,1)S(1)} %copy-done.22), channel_id=1, source_target_pairs={{0,2},{1,3},{2,0},{3,1},{4,6},{5,7},{6,4},{7,5},{8,10},{9,11},{10,... | collective-permute-start | bytes 3145736 | tf_op jit(solution)/shard_map/ppermute | solution.py:15
  254.0 85.4 %collective-permute-start.8 = (f32[2,2,2,64,768]{4,3,2,1,0:T(8,128)}, f32[2,2,2,64,768]{4,3,2,1,0:T(8,128)}, u32[]{:S(2)}, u32[]{:S(2)}) collective-permute-start(f32[2,2,2,64,768]{4,3,2,1,0:T(8,128)} %fusion.121), channel_id=1, source_target_pairs={{0,4},{4,0},{8,12},{12,8},{16,20},{20,16},{24,28},{28,24},{1,5},{5... | collective-permute-start | bytes 4718600 | tf_op jit(solution)/shard_map/ppermute | solution.py:15
  274.3 69.0 %collective-permute-start.30 = (f32[2,2,2,64,768]{4,3,2,1,0:T(8,128)}, f32[2,2,2,64,768]{4,3,2,1,0:T(8,128)}, u32[]{:S(2)}, u32[]{:S(2)}) collective-permute-start(f32[2,2,2,64,768]{4,3,2,1,0:T(8,128)} %fusion.116), channel_id=1, source_target_pairs={{0,4},{4,0},{8,12},{12,8},{16,20},{20,16},{24,28},{28,24},{1,5},{5... | collective-permute-start | bytes 4718600 | tf_op jit(solution)/shard_map/ppermute | solution.py:15
  280.4 66.4 %collective-permute-start.52 = (f32[2,2,2,64,768]{4,3,2,1,0:T(8,128)}, f32[2,2,2,64,768]{4,3,2,1,0:T(8,128)}, u32[]{:S(2)}, u32[]{:S(2)}) collective-permute-start(f32[2,2,2,64,768]{4,3,2,1,0:T(8,128)} %fusion.111), channel_id=1, source_target_pairs={{0,4},{4,0},{8,12},{12,8},{16,20},{20,16},{24,28},{28,24},{1,5},{5... | collective-permute-start | bytes 4718600 | tf_op jit(solution)/shard_map/ppermute | solution.py:15
  345.2 46.0 %collective-permute-start.31 = (f32[2,2,64,768]{3,2,0,1:T(8,128)S(1)}, f32[2,2,64,768]{3,2,0,1:T(8,128)S(1)}, u32[]{:S(2)}, u32[]{:S(2)}) collective-permute-start(f32[2,2,64,768]{3,2,0,1:T(8,128)S(1)} %bitcast.617), channel_id=1, source_target_pairs={{0,8},{4,12},{8,0},{12,4},{16,24},{20,28},{24,16},{28,20},{1,9},{5... | collective-permute-start | bytes 2359304 | tf_op jit(solution)/shard_map/ppermute | solution.py:15
  348.6 58.2 %collective-permute-start.53 = (f32[2,2,64,768]{3,2,0,1:T(8,128)S(1)}, f32[2,2,64,768]{3,2,0,1:T(8,128)S(1)}, u32[]{:S(2)}, u32[]{:S(2)}) collective-permute-start(f32[2,2,64,768]{3,2,0,1:T(8,128)S(1)} %bitcast.618), channel_id=1, source_target_pairs={{0,8},{4,12},{8,0},{12,4},{16,24},{20,28},{24,16},{28,20},{1,9},{5... | collective-permute-start | bytes 2359304 | tf_op jit(solution)/shard_map/ppermute | solution.py:15
  366.1 41.0 %collective-permute-start.10 = (f32[2,64,768]{2,1,0:T(8,128)S(1)}, f32[2,64,768]{2,1,0:T(8,128)S(1)}, u32[]{:S(2)}, u32[]{:S(2)}) collective-permute-start(f32[2,64,768]{2,1,0:T(8,128)S(1)} %dynamic-slice_bitcast_fusion.28), channel_id=1, source_target_pairs={{0,16},{4,20},{8,24},{12,28},{16,0},{20,4},{24,8},{28,12},{1,17},{... | collective-permute-start | bytes 1179656 | tf_op jit(solution)/shard_map/ppermute | solution.py:15
  (123 other events, 1393.2 us)
